TPU v7x, 32 devices: a whole 2x2x4 slice. The times are simulated.
32 devices in a mesh: sta: 16 (over z, x, core), tpl: 2 (over y).
Axes of the slice: x: 2, y: 2, z: 4, core: 2. Of those that a mesh axis runs over, the one named last changes fastest.
Arguments:
- waveform: bfloat16 [16, 3, 4279], P('sta'), may hold values from -150 to 150
- templates: bfloat16 [128, 16, 1536], P('tpl', 'sta'), may hold values from -6 to 6
- lags: int32 [128, 16], P('tpl', 'sta'), may hold values from 0 to 3000
- present: int32 [128, 16], P('tpl', 'sta'), may hold values 0 or 1
Outputs:
- score: float32 [768, 128], P('sta', 'tpl')
- scale_mad: float32 [128], P('tpl')
- peak: float32 [768], P('sta')
All inputs are finite; a program needn't handle non-finite values. No bound on the sum of `present` on one device may be relied on, other than what follows from the above.
Results may differ from a plain program's by a relative error of at most 0.0003.
Values may be sent and summed in bfloat16 or wider, within the bound.
No kernel may reach another device: no remote copies, remote signals or barrier semaphores. Data moves between devices by JAX's collectives and lax.ppermute only.
A program may use at most 64 MiB of HBM per device.

v0:
```python
import jax
import jax.numpy as jnp
from jax import lax
from jax.sharding import PartitionSpec as P

LEN = 512
LAG = 3000
BINS = 1024
TOUT_DEV = 48


def toeplitz_rows(record, length, columns):
    count = record.shape[1]
    chans = record.shape[0]
    tiled = jnp.broadcast_to(record[:, None, :], (chans, length + 1, count))
    tiled = tiled.reshape(chans, (length + 1) * count)[:, : length * (count + 1)]
    tiled = tiled.reshape(chans, length, count + 1)[:, :, :columns]
    return tiled.reshape(chans * length, columns)


def shift_rows(block, offsets, count):
    return jax.vmap(lambda row, offset: lax.dynamic_slice_in_dim(row, offset, count))(
        block, offsets
    )


def hat_counts(values, nbins):
    width = 512.0 / nbins
    ncols = values.shape[1]
    position = jnp.clip(jnp.abs(values) / width - 0.5, 0.0, nbins - 1.0)
    lower = jnp.minimum(jnp.floor(position), nbins - 2.0)
    weight = position - lower
    index = lower.astype(jnp.int32) + nbins * jnp.arange(ncols, dtype=jnp.int32)[None, :]
    flat_index = index.reshape(-1)
    flat_weight = weight.reshape(-1)
    counts = jax.ops.segment_sum(1.0 - flat_weight, flat_index, num_segments=ncols * nbins)
    counts = counts + jax.ops.segment_sum(flat_weight, flat_index + 1, num_segments=ncols * nbins)
    return counts.reshape(ncols, nbins)


def median_abs(counts, halfway):
    width = 512.0 / counts.shape[1]
    running = jnp.cumsum(counts, axis=1)
    earlier = running - counts
    share = jnp.clip((halfway - earlier) / jnp.maximum(counts, 1.0), 0.0, 1.0)
    return width * jnp.sum(share, axis=1)


def correlate_record(record, pattern, scaling, span):
    block_rows = 1024
    blocks = -(-span // block_rows)
    padded = jnp.pad(record, ((0, 0), (0, blocks * block_rows + LEN - record.shape[1])))

    def correlate(number, corr):
        begin = number * block_rows
        segment = lax.dynamic_slice_in_dim(padded, begin, block_rows + LEN, 1)
        columns = toeplitz_rows(segment, LEN, block_rows)
        result = jnp.dot(pattern, columns, preferred_element_type=jnp.float32) / scaling[:, None]
        return lax.dynamic_update_slice_in_dim(corr, result, begin, 1)

    return lax.fori_loop(
        0, blocks, correlate, jnp.zeros((pattern.shape[0], blocks * block_rows), jnp.float32)
    )


def on_device(waveform, templates, lags, present):
    stations = lax.axis_size("sta")
    total = TOUT_DEV * stations
    span = total + LAG
    record = waveform[0]
    pattern = templates[:, 0, :]
    offsets = lags[:, 0]
    member = present[:, 0].astype(jnp.float32)
    scaling = jnp.sqrt(jnp.sum(pattern.astype(jnp.float32) ** 2, axis=1) + 1e-06)
    corr = correlate_record(record, pattern, scaling, span)
    moved = shift_rows(corr, offsets, total) * member[:, None]
    arrived = lax.all_to_all(moved, "sta", split_axis=1, concat_axis=0, tiled=True)
    owned = jnp.sum(arrived.reshape(stations, moved.shape[0], TOUT_DEV), axis=0)
    stack = owned.T
    counts = hat_counts(stack, BINS)
    summed = lax.psum(counts, "sta")
    median = median_abs(summed, 0.5 * total)
    scale_mad = 1.4826 * median
    score = stack / scale_mad[None, :]
    local_best = jnp.max(score, axis=1)
    peak = lax.pmax(local_best, "tpl")
    return (score, scale_mad, peak)


def solution(mesh):
    placed = (P("sta", None, None), P("tpl", "sta", None), P("tpl", "sta"), P("tpl", "sta"))
    return jax.shard_map(
        on_device,
        mesh=mesh,
        in_specs=placed,
        out_specs=(P("sta", "tpl"), P("tpl"), P("sta")),
        check_vma=False,
    )
```

profile of v0, /device:TPU:0, one launch (start us, length us, event | category | flops | bytes accessed | tf_op | source)
XLA Modules:
  0.0 590.2 jit_solution(13781624587618451553)
XLA Ops:
  10.1 143.2 %while.14 = (s32[]{:T(128)}, f32[64,4096]{1,0:T(8,128)}, bf16[3,4608]{1,0:T(4,128)(2,1)S(1)}, bf16[64,1536]{1,0:T(8,128)(2,1)}, f32[64]{0:T(128)S(1)}, /*index=5...) while((s32[]{:T(128)}, f32[64,4096]{1,0:T(8,128)}, bf16[3,4608]{1,0:T(4,128)(2,1)S(1)}, ...), condition=%wide.region_2.3_spmd, body=%wide.region_1.2_spmd.sunk | while | flops 201392128 | bytes 56369640 | solution.py:61
  10.1 2.5 broadcast_bitcast_fusion.2
  12.6 5.6 copy.35
  18.2 3.9 slice.42
  22.1 9.1 %reshape.114 = bf16[2360832]{0:T(1024)(128)(2,1)} reshape(bf16[3,786944]{1,0:T(4,128)(2,1)} %slice.42) | data formatting | bytes 9443328 | tf_op jit(solution)/shard_map/while
  31.2 11.4 %reshape.115 = bf16[3,512,1537]{2,1,0:T(8,128)(2,1)} reshape(bf16[2360832]{0:T(1024)(128)(2,1)} %reshape.114) | data formatting | bytes 9443328 | tf_op jit(solution)/shard_map/while/body/eval_jaxpr/reshape | solution.py:17
  45.9 2.5 broadcast_bitcast_fusion.2
  48.4 5.6 copy.35
  54.0 3.9 slice.42
  57.9 9.1 %reshape.114 = bf16[2360832]{0:T(1024)(128)(2,1)} reshape(bf16[3,786944]{1,0:T(4,128)(2,1)} %slice.42) | data formatting | bytes 9443328 | tf_op jit(solution)/shard_map/while
  67.0 11.4 %reshape.115 = bf16[3,512,1537]{2,1,0:T(8,128)(2,1)} reshape(bf16[2360832]{0:T(1024)(128)(2,1)} %reshape.114) | data formatting | bytes 9443328 | tf_op jit(solution)/shard_map/while/body/eval_jaxpr/reshape | solution.py:17
  81.7 2.5 broadcast_bitcast_fusion.2
  84.2 5.6 copy.35
  89.8 3.9 slice.42
  93.7 9.1 %reshape.114 = bf16[2360832]{0:T(1024)(128)(2,1)} reshape(bf16[3,786944]{1,0:T(4,128)(2,1)} %slice.42) | data formatting | bytes 9443328 | tf_op jit(solution)/shard_map/while
  102.8 11.4 %reshape.115 = bf16[3,512,1537]{2,1,0:T(8,128)(2,1)} reshape(bf16[2360832]{0:T(1024)(128)(2,1)} %reshape.114) | data formatting | bytes 9443328 | tf_op jit(solution)/shard_map/while/body/eval_jaxpr/reshape | solution.py:17
  117.5 2.5 broadcast_bitcast_fusion.2
  120.0 5.6 copy.35
  125.6 3.9 slice.42
  129.5 9.1 %reshape.114 = bf16[2360832]{0:T(1024)(128)(2,1)} reshape(bf16[3,786944]{1,0:T(4,128)(2,1)} %slice.42) | data formatting | bytes 9443328 | tf_op jit(solution)/shard_map/while
  138.6 11.4 %reshape.115 = bf16[3,512,1537]{2,1,0:T(8,128)(2,1)} reshape(bf16[2360832]{0:T(1024)(128)(2,1)} %reshape.114) | data formatting | bytes 9443328 | tf_op jit(solution)/shard_map/while/body/eval_jaxpr/reshape | solution.py:17
  153.3 260.9 %while.15 = (s32[]{:T(128)}, f32[64,4096]{1,0:T(8,128)}, s32[64,2]{0,1:T(2,128)S(1)}, f32[64,768]{1,0:T(8,128)}, s32[]{:T(128)}, /*index=5*/s32[]{:T(128)}) while((s32[]{:T(128)}, f32[64,4096]{1,0:T(8,128)}, s32[64,2]{0,1:T(2,128)S(1)}, f32[64,768]{1,0:T(8,128)}, s32[]{:T(128)}, /*index=5*/s32[]{:T(128)}) %tuple.53), condition=%wide.while_cond, body=%wide.while_body.sunk | while | flops 2 | bytes 12401 | solution.py:22
  153.9 2.1 dynamic-slice.7
  158.0 2.1 dynamic-slice.7
  170.2 2.1 dynamic-slice.7
  174.3 2.1 dynamic-slice.7
  416.8 7.4 %all-to-all-start = ((f32[16,1,3072]{2,1,0:T(1,128)}), f32[16,1,3072]{2,1,0:T(1,128)S(1)}, u32[]{:S(2)}, u32[]{:S(2)}) async-start(f32[16,1,3072]{2,1,0:T(1,128)} %reshape.110), calls=%async_computation | async-start | bytes 393216 | tf_op jit(solution)/shard_map/all_to_all | solution.py:77
  424.2 8.9 %all-to-all-done = f32[16,1,3072]{2,1,0:T(1,128)S(1)} async-done(((f32[16,1,3072]{2,1,0:T(1,128)}), f32[16,1,3072]{2,1,0:T(1,128)S(1)}, u32[]{:S(2)}, u32[]{:S(2)}) %all-to-all-start) | async-done | bytes 196640 | tf_op jit(solution)/shard_map/all_to_all | solution.py:77
  435.1 32.6 %scatter_custom_fusion = f32[65536]{0:T(1024)S(1)} fusion(s32[6144]{0:T(1024)S(1)} %bitcast.72, f32[6144]{0:T(1024)S(1)} %pad_maximum_fusion, f32[]{:T(128)} %constant.61.clone.1), kind=kCustom, calls=%fused_computation.15 | custom fusion | flops 6144 | bytes 262148 | tf_op jit(solution)/shard_map/add | solution.py:37
  468.6 87.8 %all-reduce.3.cloned.1.call-done = f32[64,1024]{1,0:T(8,128)} async-done(((f32[64,1024]{1,0:T(8,128)}), f32[64,1024]{1,0:T(8,128)}) %all-reduce.3.cloned.1.call-update) | async-done | bytes 262160 | tf_op jit(solution)/shard_map/psum | solution.py:81
  557.4 18.0 %reduce-window.6 = f32[64,8,128]{2,1,0:T(8,128)S(1)} reduce-window(f32[64,8,128]{2,1,0:T(8,128)S(1)} %bitcast.70, f32[]{:T(128)} %constant.61.clone.1), window={size=1x1x128 pad=0_0x0_0x127_0}, to_apply=%region_6.7 | reduce-window | flops 8323072 | bytes 524292 | tf_op jit(solution)/shard_map/reduce-window
  577.9 5.4 pmax.7
  (323 shorter events, 277.4 us)
Async XLA Ops:
  10.1 143.2 %copy-start.2 = (s32[64,1]{0,1:T(1,128)S(1)}, s32[64,1]{0,1:T(1,128)}, u32[]{:S(2)}) copy-start(s32[64,1]{0,1:T(1,128)} %param.8) | copy-start | bytes 772
  10.1 405.3 %copy-start.3 = (s32[64,1]{0,1:T(1,128)S(1)}, s32[64,1]{0,1:T(1,128)}, u32[]{:S(2)}) copy-start(s32[64,1]{0,1:T(1,128)} %param.9) | copy-start | bytes 772
  42.6 2.0 slice-start
  42.6 2.0 copy-start
  78.4 2.0 slice-start
  78.4 2.0 copy-start
  114.1 2.0 slice-start
  114.2 2.0 copy-start
  149.9 2.0 slice-start
  149.9 2.0 copy-start
  416.8 16.4 %all-to-all-start = ((f32[16,1,3072]{2,1,0:T(1,128)}), f32[16,1,3072]{2,1,0:T(1,128)S(1)}, u32[]{:S(2)}, u32[]{:S(2)}) async-start(f32[16,1,3072]{2,1,0:T(1,128)} %reshape.110), calls=%async_computation | async-start | bytes 393216 | tf_op jit(solution)/shard_map/all_to_all | solution.py:77
  424.2 132.2 %all-reduce.3.cloned.1.call-start = ((), (), s32[]{:S(2)}) async-start(), calls=%async_computation.1 | async-start | bytes 524288 | tf_op jit(solution)/shard_map/psum | solution.py:81
  577.1 6.2 %copy-start.1 = (f32[64]{0:T(128)}, f32[64]{0:T(128)S(1)}, u32[]{:S(2)}) copy-start(f32[64]{0:T(128)S(1)} %broadcast_multiply_fusion.1) | copy-start | bytes 772
Sparse Core Ops, SparseCore 0:
  468.7 87.6 all-reduce.2
where the time goes:
time: 600 us; the launch traced here: 590 us
  local copies, waits for them, and re-layouts  406 us (68%)
  waiting for transfers between devices  96.7 us (16%)
  other arithmetic  54.5 us (9%)
  between operations  14.2 us (2%)
  starting transfers between devices  7.43 us (1%)
    gather x256, local copies, waits for them, and re-layouts  261 us
    psum x1, waiting for transfers between devices, on_device(): summed = lax.psum(counts, 'sta')  87.8 us
    while x20, local copies, waits for them, and re-layouts  68.7 us
    reshape x4, local copies, waits for them, and re-layouts, toeplitz_rows(): tiled = tiled.reshape(chans, length, count + 1)[:, :, :columns]  45.5 us
    add x1, other arithmetic, hat_counts(): counts + jax.ops.segment_sum(flat_weight, flat_index + 1, num_segments=nc...  32.6 us
    another operation x4, other arithmetic  18.2 us
    slice x4, local copies, waits for them, and re-layouts, toeplitz_rows(): tiled = tiled.reshape(chans, (length + 1) * count)[:, :length * (count + 1)]  15.5 us
  transfers between devices with their start and end apart: 2, of which 2 were waited for; matrix products, arithmetic and copies ran while one was open for 0% of the time, Pallas kernels for 0%

commit v1 on v0

v1 whole, which is shorter than its diff:
```python
import jax
import jax.numpy as jnp
from jax import lax
from jax.experimental import pallas as pl
from jax.experimental.pallas import tpu as pltpu
from jax.sharding import PartitionSpec as P

LEN = 512
LAG = 3000
BINS = 1024
TOUT_DEV = 48
LANES = 128
TILE = 256


def ceil_to(value, step):
    return -(-value // step) * step


def correlate(waveform, pattern, offsets, present, total):
    chans, samples = waveform.shape[1:]
    ntpl, width = pattern.shape
    taps = LEN // LANES
    rows = total // LANES
    fetch = ceil_to(rows + 1, 8)
    columns = ceil_to(total + LAG, TILE)
    held = ceil_to(max(LAG // LANES + fetch, columns // LANES), 8)
    built = columns + LEN - LANES
    padded = ceil_to(max(built + LANES, samples), LANES)

    def kernel(lag_ref, wave_ref, pattern_ref, present_ref, out_ref, line_ref, hankel_ref, corr_ref):
        line_ref[...] = jnp.zeros_like(line_ref)
        line_ref[0:chans, 0:samples] = wave_ref[0].astype(jnp.float32)
        pattern_in = pattern_ref[...]
        wide = pattern_in.astype(jnp.float32)
        tnorm = jnp.sqrt(jnp.sum(wide * wide, axis=1, keepdims=True) + 1e-06)
        factor = present_ref[...].astype(jnp.float32) / tnorm
        step = lax.broadcasted_iota(jnp.int32, (8, padded), 0)
        for c in range(chans):
            base = jnp.broadcast_to(line_ref[c : c + 1, :], (8, padded))
            for k in (1, 2, 4):
                base = jnp.where((step & k) != 0, pltpu.roll(base, padded - k, 1), base)
            for h in range(LANES // 16):
                low = base if h == 0 else pltpu.roll(base, padded - 16 * h, 1)
                high = pltpu.roll(base, padded - 16 * h - 8, 1)
                both = jnp.concatenate([low, high], axis=0).astype(jnp.bfloat16)
                hankel_ref[c, 16 * h : 16 * h + 16, :] = both[:, :built]
        for n in range(columns // TILE):
            right = jnp.concatenate(
                [
                    hankel_ref[c, :, n * TILE + a * LANES : n * TILE + a * LANES + TILE]
                    for c in range(chans)
                    for a in range(taps)
                ],
                axis=0,
            )
            corr = jnp.dot(pattern_in, right, preferred_element_type=jnp.float32) * factor
            for part in range(TILE // LANES):
                place = n * (TILE // LANES) + part
                corr_ref[pl.ds(place, ntpl, stride=held), :] = corr[:, part * LANES : (part + 1) * LANES]
        lane = lax.broadcasted_iota(jnp.int32, (fetch, LANES), 1)
        for t in range(ntpl):
            lag = lag_ref[t]
            block = lag // LANES
            rest = lag - block * LANES
            got = corr_ref[pl.ds(t * held + block, fetch), :]
            turned = pltpu.roll(got, LANES - rest, 1)
            below = pltpu.roll(turned, fetch - 1, 0)
            moved = jnp.where(lane < LANES - rest, turned, below)
            out_ref[t * rows : (t + 1) * rows, :] = moved[0:rows, :]

    return pl.pallas_call(
        kernel,
        out_shape=jax.ShapeDtypeStruct((ntpl * rows, LANES), jnp.float32),
        in_specs=[
            pl.BlockSpec(memory_space=pltpu.SMEM),
            pl.BlockSpec(memory_space=pltpu.VMEM),
            pl.BlockSpec(memory_space=pltpu.VMEM),
            pl.BlockSpec(memory_space=pltpu.VMEM),
        ],
        out_specs=pl.BlockSpec(memory_space=pltpu.VMEM),
        scratch_shapes=[
            pltpu.VMEM((8, padded), jnp.float32),
            pltpu.VMEM((chans, LANES, built), jnp.bfloat16),
            pltpu.VMEM((ntpl * held, LANES), jnp.float32),
        ],
        name="correlate",
    )(offsets, waveform, pattern, present)


def score_rows(arrived, stations, groups, total):
    rows = total // LANES
    count = arrived.shape[0] // stations
    ntpl = count // rows
    width = 512.0 / BINS

    def kernel(in_ref, out_ref, stack_ref):
        stack = in_ref[0:count, :]
        for s in range(1, stations):
            stack = stack + in_ref[s * count : (s + 1) * count, :]
        stack_ref[...] = stack
        position = jnp.clip(jnp.abs(stack) / width - 0.5, 0.0, BINS - 1.0)
        fill = jnp.zeros((LANES - count, LANES), jnp.float32)
        turned = jnp.transpose(jnp.concatenate([position, fill], axis=0))
        bins = lax.broadcasted_iota(jnp.int32, (8, BINS), 1).astype(jnp.float32)
        sums = []
        for t in range(ntpl):
            acc = jnp.zeros((8, BINS), jnp.float32)
            for m in range(rows):
                for r in range(LANES // 8):
                    at = t * rows + m
                    spot = turned[8 * r : 8 * r + 8, at : at + 1]
                    acc = acc + jnp.clip(bins - spot, 0.0, 1.0)
            sums.append(jnp.sum(acc, axis=0, keepdims=True))
        before = jnp.concatenate(sums, axis=0) if ntpl > 1 else sums[0]
        last = lax.broadcasted_iota(jnp.int32, before.shape, 1) == BINS - 1
        cum = jnp.where(last, float(total), pltpu.roll(before, BINS - 1, 1))
        share = jnp.clip((0.5 * total - before) / jnp.maximum(cum - before, 1.0), 0.0, 1.0)
        scale = 1.4826 * (width * jnp.sum(share, axis=1, keepdims=True))
        score = jnp.concatenate(
            [stack_ref[pl.ds(m, ntpl, stride=rows), :] for m in range(rows)], axis=1
        ) / scale
        best = jnp.broadcast_to(jnp.max(score, axis=0, keepdims=True), score.shape)
        lane = lax.broadcasted_iota(jnp.int32, (ntpl, LANES), 1)
        for i in range(stations):
            begin = i * TOUT_DEV
            mine = score if begin == 0 else pltpu.roll(score, total - begin, 1)
            tops = pltpu.roll(best, (total + TOUT_DEV - begin) % total, 1)
            block = jnp.where(lane < TOUT_DEV, mine[:, :LANES], tops[:, :LANES])
            block = jnp.where(lane < 2 * TOUT_DEV, block, scale)
            for g in range(groups):
                place = (i * groups + g) * ntpl
                out_ref[place : place + ntpl, :] = block

    return pl.pallas_call(
        kernel,
        out_shape=jax.ShapeDtypeStruct((stations * groups * ntpl, LANES), jnp.float32),
        in_specs=[pl.BlockSpec(memory_space=pltpu.VMEM)],
        out_specs=pl.BlockSpec(memory_space=pltpu.VMEM),
        scratch_shapes=[pltpu.VMEM((count, LANES), jnp.float32)],
        name="scores",
    )(arrived)


def finish(arrived, group, stations, groups):
    ntpl = arrived.shape[0] // (stations * groups)
    held = stations * ntpl

    def kernel(group_ref, in_ref, score_ref, scale_ref, peak_ref, mine_ref):
        own = group_ref[0]
        for t in range(ntpl):
            mine_ref[pl.ds(t, stations, stride=ntpl), :] = in_ref[
                pl.ds(own * ntpl + t, stations, stride=groups * ntpl), :
            ]
        mine = mine_ref[...]
        if held < LANES:
            mine = jnp.concatenate([mine, jnp.zeros((LANES - held, LANES), jnp.float32)], axis=0)
        turned = jnp.transpose(mine)
        score_ref[...] = turned[0:TOUT_DEV, 0:held]
        scale_ref[...] = turned[2 * TOUT_DEV : 2 * TOUT_DEV + 1, 0:held]
        best = jnp.max(in_ref[...], axis=0, keepdims=True)
        peak_ref[...] = pltpu.roll(jnp.broadcast_to(best, (8, LANES)), LANES - TOUT_DEV, 1)[0:1, 0:TOUT_DEV]

    return pl.pallas_call(
        kernel,
        out_shape=(
            jax.ShapeDtypeStruct((TOUT_DEV, held), jnp.float32),
            jax.ShapeDtypeStruct((1, held), jnp.float32),
            jax.ShapeDtypeStruct((1, TOUT_DEV), jnp.float32),
        ),
        in_specs=[pl.BlockSpec(memory_space=pltpu.SMEM), pl.BlockSpec(memory_space=pltpu.VMEM)],
        out_specs=(pl.BlockSpec(memory_space=pltpu.VMEM),) * 3,
        scratch_shapes=[pltpu.VMEM((held, LANES), jnp.float32)],
        name="finish",
    )(group, arrived)


def on_device(waveform, templates, lags, present):
    stations = lax.axis_size("sta")
    groups = lax.axis_size("tpl")
    total = TOUT_DEV * stations
    moved = correlate(waveform, templates[:, 0, :], lags[:, 0], present, total)
    arrived = lax.all_to_all(moved, "sta", split_axis=0, concat_axis=0, tiled=True)
    scored = score_rows(arrived, stations, groups, total)
    spread = lax.all_to_all(scored, ("sta", "tpl"), split_axis=0, concat_axis=0, tiled=True)
    group = lax.axis_index("tpl").astype(jnp.int32).reshape(1)
    score, scale_mad, peak = finish(spread, group, stations, groups)
    return (score, scale_mad.reshape(-1), peak.reshape(-1))


def solution(mesh):
    placed = (P("sta", None, None), P("tpl", "sta", None), P("tpl", "sta"), P("tpl", "sta"))
    return jax.shard_map(
        on_device,
        mesh=mesh,
        in_specs=placed,
        out_specs=(P("sta", "tpl"), P("tpl"), P("sta")),
        check_vma=False,
    )
```

time: 600 us -> 40.5 us (0.07); the launches traced: 590 us -> 40.2 us
  local copies, waits for them, and re-layouts: 406 us -> 1.96 us
  waiting for transfers between devices: 96.7 us -> 7.6 us
  other arithmetic: 54.5 us -> 0 us
  between operations: 14.2 us -> 0.65 us
  blocking collectives: 5.41 us -> 16.4 us
  Pallas kernels: 0 us -> 10.9 us
    gather x257 -> x0, local copies, waits for them, and re-layouts: 262 us -> none
    psum x1 -> x0, waiting for transfers between devices: 87.8 us -> none  [on_device(): summed = lax.psum(counts, 'sta')]
    while x20 -> x0, local copies, waits for them, and re-layouts: 68.7 us -> none
    reshape x6 -> x0, local copies, waits for them, and re-layouts: 46.3 us -> none  [the longest x4 45.5 us: toeplitz_rows(): tiled = tiled.reshape(chans, length, count + 1)[:, :, :columns]]
    add x3 -> x0, other arithmetic: 32.7 us -> none  [the longest x1 32.6 us: hat_counts(): counts + jax.ops.segment_sum(flat_weight, flat_index + 1, num_segments=nc...]
    slice x12 -> x0, local copies, waits for them, and re-layouts: 23.4 us -> none  [the longest x4 15.5 us: toeplitz_rows(): tiled = tiled.reshape(chans, (length + 1) * count)[:, :length * (count + 1)]]
    another operation x4 -> x0, other arithmetic: 18.2 us -> none
    all_to_all x0 -> x1, blocking collectives: none -> 16.4 us  [on_device(): lax.all_to_all(moved, 'sta', split_axis=0, concat_axis=0, tiled=True)]
  transfers between devices with their start and end apart: 2 -> 1, of which waited for: 2 -> 1; matrix products, arithmetic and copies ran while one was open for 0% -> 0% of each run, Pallas kernels for 0% -> 0%
where the time goes in v1:
time: 40.5 us; the launch traced here: 40.2 us
  blocking collectives  16.4 us (40%)
  Pallas kernels  10.9 us (27%)
  waiting for transfers between devices  7.6 us (19%)
  starting transfers between devices  2.55 us (6%)
  local copies, waits for them, and re-layouts  1.96 us (5%)
  between operations  0.65 us (2%)
    all_to_all x1, blocking collectives, on_device(): lax.all_to_all(moved, 'sta', split_axis=0, concat_axis=0, tiled=True)  16.4 us
    all_to_all x1, waiting for transfers between devices, on_device(): lax.all_to_all(scored, ('sta', 'tpl'), split_axis=0, concat_axis=0, tiled...  7.6 us
    pallas_call x1, Pallas kernels, correlate(): pl.pallas_call(kernel, out_shape=jax.ShapeDtypeStruct((ntpl * rows, LANES...  6.07 us
    pallas_call x1, Pallas kernels, score_rows(): pl.pallas_call(kernel, out_shape=jax.ShapeDtypeStruct((stations * groups...  3.31 us
    all_to_all x1, starting transfers between devices, on_device(): lax.all_to_all(scored, ('sta', 'tpl'), split_axis=0, concat_axis=0, tiled...  2.55 us
    unnamed x3, local copies, waits for them, and re-layouts  1.96 us
    pallas_call x1, Pallas kernels, finish(): pl.pallas_call(kernel, out_shape=(jax.ShapeDtypeStruct((TOUT_DEV, held),...  1.56 us
  transfers between devices with their start and end apart: 1, of which 1 were waited for; matrix products, arithmetic and copies ran while one was open for 0% of the time, Pallas kernels for 0%

profile of v1, /device:TPU:0, one launch (start us, length us, event | category | flops | bytes accessed | tf_op | source)
XLA Modules:
  0.0 40.2 jit_solution(7325070913985356280)
XLA Ops:
  0.6 1.3 %copy.7.present_ref = s32[64,1]{1,0:T(8,128)} copy(s32[64,1]{0,1:T(1,128)} %param.7) | data formatting | bytes 512 | tf_op args[3]
  2.0 6.1 %correlate.1 = f32[384,128]{1,0:T(8,128)} custom-call(s32[64]{0:T(128)} %bitcast.14, bf16[1,3,4279]{2,1,0:T(4,128)(2,1)} %wave_ref.1, bf16[64,1536]{1,0:T(8,128)(2,1)} %bitcast.13, s32[64,1]{1,0:T(8,128)} %copy.7.present_ref), custom_call_target="tpu_custom_call" | custom-call | tf_op jit(solution)/shard_map/correlate/pallas_call | solution.py:72
  8.0 16.4 %all_to_all.22 = f32[16,24,128]{2,1,0:T(8,128)} all-to-all(f32[16,24,128]{2,1,0:T(8,128)} %bitcast.9), channel_id=1, replica_groups=mesh['sta'=16,'tpl'=2] {'sta'}, dimensions={0} | all-to-all | bytes 393216 | tf_op jit(solution)/shard_map/all_to_all | solution.py:183
  24.5 3.3 %scores.1 = f32[128,128]{1,0:T(8,128)} custom-call(f32[384,128]{1,0:T(8,128)} %bitcast.10), custom_call_target="tpu_custom_call" | custom-call | tf_op jit(solution)/shard_map/scores/pallas_call | solution.py:135
  27.8 2.6 %all-to-all-start.1 = ((f32[32,4,128]{2,1,0:T(4,128)}), f32[32,4,128]{2,1,0:T(4,128)S(1)}, u32[]{:S(2)}, u32[]{:S(2)}) async-start(f32[32,4,128]{2,1,0:T(4,128)} %bitcast.12), calls=%async_computation.1 | async-start | bytes 131072 | tf_op jit(solution)/shard_map/all_to_all | solution.py:185
  30.4 7.6 %all-to-all-done.1 = f32[32,4,128]{2,1,0:T(4,128)S(1)} async-done(((f32[32,4,128]{2,1,0:T(4,128)}), f32[32,4,128]{2,1,0:T(4,128)S(1)}, u32[]{:S(2)}, u32[]{:S(2)}) %all-to-all-start.1) | async-done | bytes 65568 | tf_op jit(solution)/shard_map/all_to_all | solution.py:185
  38.0 0.0 copy-start
  38.0 0.6 %copy-done = f32[32,4,128]{2,1,0:T(4,128)} copy-done((f32[32,4,128]{2,1,0:T(4,128)}, f32[32,4,128]{2,1,0:T(4,128)S(1)}, u32[]{:S(2)}) %copy-start) | copy-done | bytes 65560
  38.6 1.6 %finish.1 = (f32[48,64]{1,0:T(8,128)}, f32[1,64]{1,0:T(1,128)}, f32[1,48]{1,0:T(1,128)}) custom-call(s32[1]{0:T(128)} %bitcast.group_ref, f32[128,128]{1,0:T(8,128)} %bitcast.11), custom_call_target="tpu_custom_call" | custom-call | tf_op jit(solution)/shard_map/finish/pallas_call | solution.py:164
Async XLA Ops:
  27.8 10.2 %all-to-all-start.1 = ((f32[32,4,128]{2,1,0:T(4,128)}), f32[32,4,128]{2,1,0:T(4,128)S(1)}, u32[]{:S(2)}, u32[]{:S(2)}) async-start(f32[32,4,128]{2,1,0:T(4,128)} %bitcast.12), calls=%async_computation.1 | async-start | bytes 131072 | tf_op jit(solution)/shard_map/all_to_all | solution.py:185
  38.0 0.6 %copy-start = (f32[32,4,128]{2,1,0:T(4,128)}, f32[32,4,128]{2,1,0:T(4,128)S(1)}, u32[]{:S(2)}) copy-start(f32[32,4,128]{2,1,0:T(4,128)S(1)} %all-to-all-done.1) | copy-start | bytes 196612
